TPU v7x, 32 devices: a whole 2x2x4 slice. The times are simulated.
32 devices in a mesh: span: 32 (over z, y, x, core).
Axes of the slice: x: 2, y: 2, z: 4, core: 2. Of those that a mesh axis runs over, the one named last changes fastest.
Arguments:
- random_slabs: bfloat16 [1024, 4, 3, 2048], P('span'), may hold values from -6 to 6
- span_weights: float32 [513], replicated, may hold values from 0.1 to 2
- wall_filter: bfloat16 [2048, 2048], replicated, may hold values from -0.125 to 0.125
- prev_state: float32 [1024, 3, 2048], P('span'), may hold values from -6 to 6
- time_scale: float32 [3, 2048], replicated, may hold values from 1 to 32
- mean_velocity: float32 [2048], replicated, may hold values from 0 to 2
- lund_diag: float32 [3, 2048], replicated, may hold values from 0.3 to 3
- lund_off: float32 [3, 2048], replicated, may hold values from -1 to 1
Outputs:
- velocity: bfloat16 [1024, 4, 3, 2048], P('span')
- new_state: float32 [1024, 3, 2048], P('span')
All inputs are finite; a program needn't handle non-finite values.
Results may differ from a plain program's by a relative error of at most 0.0051.
Values may be sent and summed in bfloat16 or wider, within the bound.
A program may use at most 128 MiB of HBM per device.

v0:
```python
import functools

import jax
import jax.numpy as jnp
from jax import lax
from jax.experimental import pallas as pl
from jax.experimental.pallas import tpu as pltpu
from jax.sharding import PartitionSpec as P

LANES = 256
MESH = pl.DeviceIdType.MESH


def peer_of(step, me, count):
    away = count // 2 + (1 - 2 * (step % 2)) * ((step + 1) // 2)
    return lax.rem(me + away, count)


def exchange_kernel(
    count,
    rows,
    width,
    pairs,
    parts,
    slim,
    reach,
    slab_ref,
    taps_ref,
    wall_ref,
    prev_ref,
    scale_ref,
    mean_ref,
    diag_ref,
    off_ref,
    vel_ref,
    state_ref,
    x_ref,
    wide,
    summed,
    back,
    band,
    wall,
    early,
    decay,
    inject,
    wall_sem,
    out_sem,
    in_sem,
    back_out_sem,
    back_in_sem,
):
    me = lax.axis_index("span")
    per = width // slim
    group = pairs // parts
    blocks = count * rows // reach

    wall_copy = pltpu.make_async_copy(wall_ref, wall, wall_sem)
    wall_copy.start()

    barrier = pltpu.get_barrier_semaphore()

    @pl.loop(0, count - 1)
    def _(step):
        pl.semaphore_signal(
            barrier, inc=1, device_id=(peer_of(step, me, count),), device_id_type=MESH
        )

    def relayout(part):
        for pair in range(part * group, (part + 1) * group):
            x_ref[pair] = slab_ref[:, pair % 3, pair // 3, :]

    relayout(0)
    pl.semaphore_wait(barrier, count - 1)

    half = count // 2
    side = per // 2
    ours = me // half

    def columns(part, owner):
        place = owner % half
        start = pl.multiple_of((owner // half * side + place % side) * slim, slim)
        return part * group + place // side, pl.ds(start, slim)

    for part in range(parts):
        if part:
            relayout(part)

        @pl.loop(0, count - 1)
        def _(step):
            peer = peer_of(step, me, count)
            pair, span = columns(part, peer)
            pltpu.make_async_remote_copy(
                src_ref=x_ref.at[pair, :, span],
                dst_ref=wide.at[part, me],
                send_sem=out_sem.at[part],
                recv_sem=in_sem.at[part],
                device_id=(peer,),
                device_id_type=MESH,
            ).start()

        pair, span = columns(part, me)
        pltpu.make_async_copy(x_ref.at[pair, :, span], wide.at[part, me], in_sem.at[part]).start()

    weights = jnp.concatenate(
        [taps_ref[...], jnp.zeros((3 * reach - taps_ref.shape[0],), jnp.float32)]
    ).reshape(1, 3 * reach)
    taps = weights / jnp.sqrt(jnp.sum(weights * weights))
    tall = jnp.broadcast_to(taps, (16, 3 * reach))
    line = lax.broadcasted_iota(jnp.int32, (16, 3 * reach), 0)
    for bit in range(4):
        tall = jnp.where((line // (1 << bit)) % 2 == 1, pltpu.roll(tall, 1 << bit, 1), tall)

    @pl.loop(0, reach // 16)
    def _(step):
        first = pl.multiple_of(step * 16, 16)
        rolled = pltpu.roll(tall, first, 1)
        band[pl.ds(first, 16), :] = rolled.astype(jnp.bfloat16)

    decay[...] = jnp.exp(-jnp.pi / (2.0 * scale_ref[...]))
    inject[...] = jnp.sqrt(1.0 - jnp.exp(-jnp.pi / scale_ref[...]))
    state_ref[...] = prev_ref[...]

    for part in range(parts):
        pltpu.make_async_copy(wide.at[part], wide.at[part], in_sem.at[part]).wait()
        share = reach // rows
        for block in range(blocks):
            total = jnp.zeros((reach, slim), jnp.float32)
            for shift in range(3):
                source = (block - 1 + shift) % blocks
                chunk = wide[part, source * share : (source + 1) * share].reshape(reach, slim)
                total += jnp.dot(
                    band[:, shift * reach : (shift + 1) * reach],
                    chunk,
                    preferred_element_type=jnp.float32,
                )
            summed[part, block * share : (block + 1) * share] = total.astype(
                jnp.bfloat16
            ).reshape(share, rows, slim)

        pair, span = columns(part, me)

        @pl.loop(0, count - 1)
        def _(step):
            peer = peer_of(step, me, count)
            pltpu.make_async_remote_copy(
                src_ref=summed.at[part, peer],
                dst_ref=back.at[pair, :, span],
                send_sem=back_out_sem.at[part],
                recv_sem=back_in_sem.at[part, (peer // half + ours) % 2],
                device_id=(peer,),
                device_id_type=MESH,
            ).start()

        pltpu.make_async_copy(
            summed.at[part, me], back.at[pair, :, span], back_in_sem.at[part, 0]
        ).start()

    def finish(part, at, filtered):
        for local in range(group):
            pair = part * group + local
            component = pair % 3
            one = pl.ds(component, 1)
            new = decay[one, at] * state_ref[component, :, at] + inject[one, at] * filtered[local]
            state_ref[component, :, at] = new
            if component == 0:
                value = mean_ref[:, at] + diag_ref[0:1, at] * new
            elif component == 1:
                value = off_ref[0:1, at] * state_ref[0, :, at] + diag_ref[1:2, at] * new
            else:
                value = (
                    off_ref[1:2, at] * state_ref[0, :, at]
                    + off_ref[2:3, at] * state_ref[1, :, at]
                    + diag_ref[2:3, at] * new
                )
            vel_ref[pair, :, at] = value.astype(jnp.bfloat16)

    wall_copy.wait()
    tile = min(256, width)
    for part in range(parts):
        held = back.at[part * group : (part + 1) * group]
        for far in range(2):
            first = pl.multiple_of((ours + far) % 2 * (width // 2), width // 2)
            span = pl.ds(first, width // 2)
            mine = held.at[:, :, 0 : width // 2]
            pltpu.make_async_copy(mine, mine, back_in_sem.at[part, far]).wait()
            if part < parts - 1 and far == 0:
                continue

            @pl.loop(0, width // tile)
            def _(step):
                at = pl.ds(pl.multiple_of(step * tile, tile), tile)
                reading = span if part == parts - 1 else slice(None)
                filtered = lax.dot_general(
                    held[:, :, reading].reshape(group * rows, -1),
                    wall[at, reading],
                    (((1,), (1,)), ((), ())),
                    preferred_element_type=jnp.float32,
                ).reshape(group, rows, tile)
                if far == 0:
                    early[:, :, at] = filtered
                else:
                    if part == parts - 1:
                        filtered += early[:, :, at]
                    finish(part, at, filtered)

    for part in range(parts):
        sent = wide.at[part, 0 : count - 1]
        pltpu.make_async_copy(sent, sent, out_sem.at[part]).wait()
        pltpu.make_async_copy(sent, sent, back_out_sem.at[part]).wait()


def fits(count, rows, pairs, width, reach, slim):
    columns = pairs * width
    return (
        columns % (count * slim) == 0
        and (count * slim) % width == 0
        and width % (2 * slim) == 0
        and count % 2 == 0
        and rows % 16 == 0
        and reach % rows == 0
        and reach % 128 == 0
        and count * rows % reach == 0
        and count * rows // reach >= 3
    )


def exchanged(
    random_slabs,
    span_weights,
    wall_filter,
    prev_state,
    time_scale,
    mean_velocity,
    lund_diag,
    lund_off,
):
    count = lax.axis_size("span")
    rows, planes, kinds, width = random_slabs.shape
    pairs = planes * kinds
    reach = (span_weights.shape[0] - 1) // 2
    slim = LANES
    parts = pairs * width // (count * slim)
    x = random_slabs.transpose(0, 2, 1, 3)
    in_vmem = pl.BlockSpec(memory_space=pltpu.VMEM)
    velocity, state = pl.pallas_call(
        functools.partial(exchange_kernel, count, rows, width, pairs, parts, slim, reach),
        out_shape=(
            jax.ShapeDtypeStruct((pairs, rows, width), jnp.bfloat16),
            jax.ShapeDtypeStruct((kinds, rows, width), jnp.float32),
        ),
        in_specs=[in_vmem, in_vmem, pl.BlockSpec(memory_space=pl.ANY)] + [in_vmem] * 5,
        out_specs=(in_vmem, in_vmem),
        scratch_shapes=[
            pltpu.VMEM((pairs, rows, width), jnp.bfloat16),
            pltpu.VMEM((parts, count, rows, slim), jnp.bfloat16),
            pltpu.VMEM((parts, count, rows, slim), jnp.bfloat16),
            pltpu.VMEM((pairs, rows, width), jnp.bfloat16),
            pltpu.VMEM((reach, 3 * reach), jnp.bfloat16),
            pltpu.VMEM((width, width), jnp.bfloat16),
            pltpu.VMEM((pairs // parts, rows, width), jnp.float32),
            pltpu.VMEM((kinds, width), jnp.float32),
            pltpu.VMEM((kinds, width), jnp.float32),
            pltpu.SemaphoreType.DMA,
            pltpu.SemaphoreType.DMA((parts,)),
            pltpu.SemaphoreType.DMA((parts,)),
            pltpu.SemaphoreType.DMA((parts,)),
            pltpu.SemaphoreType.DMA((parts, 2)),
        ],
        compiler_params=pltpu.CompilerParams(collective_id=0, has_side_effects=True),
    )(
        x,
        span_weights,
        wall_filter,
        prev_state.transpose(1, 0, 2),
        time_scale,
        mean_velocity.reshape(1, width),
        lund_diag,
        lund_off,
    )
    velocity = velocity.reshape(planes, kinds, rows, width).transpose(2, 0, 1, 3)
    return velocity, state.transpose(1, 0, 2)


def from_partner(value, axis, bit):
    return lax.ppermute(value, axis, [(i, i ^ 1 << bit) for i in range(lax.axis_size(axis))])


def band_matrix(taps, height):
    reach = taps.shape[0]
    padded = jnp.concatenate([taps, jnp.zeros((height,), taps.dtype)])
    length = reach + height
    tiled = jnp.tile(padded, height)[: height * (length - 1)]
    return tiled.reshape(height, length - 1)


def butterfly(held, forward):
    count = lax.axis_size("span")
    device = lax.axis_index("span")
    levels = count.bit_length() - 1
    for level in range(levels - 1, -1, -1):
        groups, inner_first, targets, inner_last = held.shape
        halves = held.reshape(groups, inner_first, 2, targets // 2, inner_last)
        lower = halves[:, :, 0]
        higher = halves[:, :, 1]
        upper = device >> level & 1 == 1
        kept = jnp.where(upper, higher, lower)
        given = jnp.where(upper, lower, higher)
        if forward:
            taken = from_partner(given, "span", level)
        else:
            taken = from_partner(given, "span", level)
        first = jnp.where(upper, taken, kept)
        second = jnp.where(upper, kept, taken)
        held = jnp.stack([first, second], axis=1).reshape(
            groups * 2, inner_first, targets // 2, inner_last
        )
    return held


def body(
    random_slabs,
    span_weights,
    wall_filter,
    prev_state,
    time_scale,
    mean_velocity,
    lund_diag,
    lund_off,
):
    rows = random_slabs.shape[0]
    planes = random_slabs.shape[1]
    width = random_slabs.shape[3]
    columns = planes * 3 * width
    half = (span_weights.shape[0] - 1) // 2
    if fits(lax.axis_size("span"), rows, planes * 3, width, half, LANES):
        return exchanged(
            random_slabs,
            span_weights,
            wall_filter,
            prev_state,
            time_scale,
            mean_velocity,
            lund_diag,
            lund_off,
        )
    flat = random_slabs.reshape(rows, columns)
    scaling = jnp.sqrt(jnp.sum(span_weights * span_weights))
    taps = (span_weights / scaling).astype(jnp.bfloat16)
    reach = (span_weights.shape[0] - 1) // 2
    count = lax.axis_size("span")
    slim = columns // count
    held = butterfly(flat.reshape(1, rows, count, slim), True)
    total = rows * count
    whole = held.reshape(total, slim)
    height = min(512, total)
    matrix = band_matrix(taps, height)
    wrapped = jnp.concatenate([whole[total - reach :], whole, whole[:reach]], axis=0)

    def one_block(start):
        window = lax.dynamic_slice_in_dim(wrapped, start, height + 2 * reach, 0)
        return jnp.dot(matrix, window, preferred_element_type=jnp.float32)

    starts = jnp.arange(total // height) * height
    summed_cols = lax.map(one_block, starts).reshape(total, slim)
    rounded = summed_cols.astype(jnp.bfloat16)
    returned = butterfly(rounded.reshape(1, 1, count, rows * slim), False)
    spanned = returned.reshape(count, rows, slim).transpose(1, 0, 2).reshape(rows, planes, 3, width)
    filtered = lax.dot_general(
        spanned, wall_filter, (((3,), (1,)), ((), ())), preferred_element_type=jnp.float32
    )
    decay = jnp.exp(-jnp.pi / (2.0 * time_scale))
    inject = jnp.sqrt(1.0 - jnp.exp(-jnp.pi / time_scale))
    state = prev_state
    outputs = []
    for plane in range(planes):
        state = decay * state + inject * filtered[:, plane]
        along = state[:, 0]
        normal = state[:, 1]
        spanwise = state[:, 2]
        first = mean_velocity + lund_diag[0] * along
        second = lund_off[0] * along + lund_diag[1] * normal
        third = lund_off[1] * along + lund_off[2] * normal + lund_diag[2] * spanwise
        outputs.append(jnp.stack([first, second, third], axis=1).astype(jnp.bfloat16))
    velocity = jnp.stack(outputs, axis=1)
    return (velocity, state)


def solution(mesh):
    placed = (P("span", None, None, None), P(), P(), P("span", None, None), P(), P(), P(), P())
    return jax.shard_map(
        body,
        mesh=mesh,
        in_specs=placed,
        out_specs=(P("span", None, None, None), P("span", None, None)),
        check_vma=False,
    )
```

profile of v0, /device:TPU:0, one launch (start us, length us, event | category | flops | bytes accessed | tf_op | source)
XLA Modules:
  0.0 87.1 jit_solution(15482065532467604961)
XLA Ops:
  0.6 81.7 %shard_map.95 = (bf16[12,32,2048]{2,1,0:T(8,128)(2,1)}, f32[3,32,2048]{2,1,0:T(8,128)}) custom-call(bf16[32,3,4,2048]{3,2,1,0:T(4,128)(2,1)} %bitcast.10, f32[513]{0:T(1024)} %taps_ref.1, bf16[2048,2048]{1,0:T(8,128)(2,1)} %wall_ref.1, f32[3,32,2048]{2,1,0:T(8,128)} %bitcast.11, f32[3,2048]{1,0:T(4,128)} %scale_ref.1, f32[1,2048]{1,0:T(1,128)} %bitcast.13, ...), custom_call_target="tpu_custom_call" | custom-call | tf_op jit(solution)/shard_map/pallas_call | solution.py:245
  82.4 0.0 copy-start
  82.4 3.8 %copy.12 = bf16[4,3,32,2048]{3,0,1,2:T(4,128)(2,1)} copy(bf16[4,3,32,2048]{3,2,1,0:T(8,128)(2,1)} %bitcast.9) | data formatting | bytes 3145728 | tf_op jit(solution)/shard_map/reshape | solution.py:280
  86.2 0.0 copy-done
  86.2 0.9 %copy.14 = f32[32,3,2048]{2,0,1:T(8,128)} copy(f32[32,3,2048]{2,0,1:T(8,128)S(1)} %bitcast.12) | data formatting | bytes 1572864
Async XLA Ops:
  82.4 3.9 %copy-start = (f32[3,32,2048]{2,1,0:T(8,128)S(1)}, f32[3,32,2048]{2,1,0:T(8,128)}, u32[]{:S(2)}) copy-start(f32[3,32,2048]{2,1,0:T(8,128)} %get-tuple-element.5) | copy-start | bytes 2359300
where the time goes:
time: 87.3 us; the launch traced here: 87.1 us
  Pallas kernels  81.7 us (94%)
  local copies, waits for them, and re-layouts  4.72 us (5%)
    pallas_call x1, Pallas kernels, exchanged(): pl.pallas_call(functools.partial(exchange_kernel, count, rows, width, pai...  81.7 us
    reshape x1, local copies, waits for them, and re-layouts, exchanged(): velocity.reshape(planes, kinds, rows, width).transpose(2, 0, 1, 3)  3.84 us

commit v1 on v0

--- a/solution.py
+++ b/solution.py
@@ -8,10 +8,11 @@
 from jax.sharding import PartitionSpec as P
 
 LANES = 256
+GRANT = 32 << 20
 MESH = pl.DeviceIdType.MESH
 
 
-def peer_of(step, me, count):
+def peer_at(step, me, count):
     away = count // 2 + (1 - 2 * (step % 2)) * ((step + 1) // 2)
     return lax.rem(me + away, count)
 
@@ -20,20 +21,26 @@
     count,
     rows,
     width,
-    pairs,
-    parts,
+    planes,
+    kinds,
     slim,
     reach,
-    slab_ref,
+    slab_hbm,
+    taps_hbm,
+    wall_hbm,
+    prev_hbm,
+    scale_hbm,
+    mean_hbm,
+    diag_hbm,
+    off_hbm,
+    vel_ref,
+    state_ref,
+    slab,
     taps_ref,
-    wall_ref,
-    prev_ref,
     scale_ref,
     mean_ref,
     diag_ref,
     off_ref,
-    vel_ref,
-    state_ref,
     x_ref,
     wide,
     summed,
@@ -41,56 +48,79 @@
     band,
     wall,
     early,
+    along,
+    normal,
     decay,
     inject,
-    wall_sem,
+    load_sem,
+    slab_sem,
     out_sem,
     in_sem,
     back_out_sem,
     back_in_sem,
 ):
     me = lax.axis_index("span")
-    per = width // slim
-    group = pairs // parts
     blocks = count * rows // reach
-
-    wall_copy = pltpu.make_async_copy(wall_ref, wall, wall_sem)
-    wall_copy.start()
-
+    half = count // 2
+    ours = me // half
+
+    slab_loads = [
+        pltpu.make_async_copy(slab_hbm.at[:, kind], slab.at[kind], slab_sem.at[kind])
+        for kind in range(kinds)
+    ]
+    loads = [
+        pltpu.make_async_copy(source, target, load_sem.at[at])
+        for at, (source, target) in enumerate(
+            (
+                (taps_hbm, taps_ref),
+                (scale_hbm, scale_ref),
+                (mean_hbm, mean_ref),
+                (diag_hbm, diag_ref),
+                (off_hbm, off_ref),
+                (prev_hbm, state_ref),
+                (wall_hbm, wall),
+            )
+        )
+    ]
+    slab_loads[0].start()
     barrier = pltpu.get_barrier_semaphore()
 
     @pl.loop(0, count - 1)
     def _(step):
         pl.semaphore_signal(
-            barrier, inc=1, device_id=(peer_of(step, me, count),), device_id_type=MESH
+            barrier, inc=1, device_id=(peer_at(step, me, count),), device_id_type=MESH
         )
 
-    def relayout(part):
-        for pair in range(part * group, (part + 1) * group):
-            x_ref[pair] = slab_ref[:, pair % 3, pair // 3, :]
+    for load in slab_loads[1:]:
+        load.start()
+    for load in loads:
+        load.start()
+
+    def relayout(kind):
+        slab_loads[kind].wait()
+        for plane in range(planes):
+            x_ref[kind, plane] = slab[kind, :, plane, :]
 
     relayout(0)
     pl.semaphore_wait(barrier, count - 1)
 
-    half = count // 2
-    side = per // 2
-    ours = me // half
-
-    def columns(part, owner):
+    side = width // slim // 2
+
+    def columns(owner):
         place = owner % half
         start = pl.multiple_of((owner // half * side + place % side) * slim, slim)
-        return part * group + place // side, pl.ds(start, slim)
-
-    for part in range(parts):
+        return place // side, pl.ds(start, slim)
+
+    for part in range(kinds):
         if part:
             relayout(part)
 
         @pl.loop(0, count - 1)
         def _(step):
-            peer = peer_of(step, me, count)
-            pair, span = columns(part, peer)
+            peer = peer_at(step, me, count)
+            plane, span = columns(peer)
             pltpu.make_async_remote_copy(
-                src_ref=x_ref.at[pair, :, span],
+                src_ref=x_ref.at[part, plane, :, span],
                 dst_ref=wide.at[part, me],
                 send_sem=out_sem.at[part],
                 recv_sem=in_sem.at[part],
@@ -98,9 +128,13 @@
                 device_id_type=MESH,
             ).start()
 
-        pair, span = columns(part, me)
-        pltpu.make_async_copy(x_ref.at[pair, :, span], wide.at[part, me], in_sem.at[part]).start()
-
+        plane, span = columns(me)
+        pltpu.make_async_copy(
+            x_ref.at[part, plane, :, span], wide.at[part, me], in_sem.at[part]
+        ).start()
+
+    for load in loads:
+        load.wait()
     weights = jnp.concatenate(
         [taps_ref[...], jnp.zeros((3 * reach - taps_ref.shape[0],), jnp.float32)]
     ).reshape(1, 3 * reach)
@@ -118,9 +152,8 @@
 
     decay[...] = jnp.exp(-jnp.pi / (2.0 * scale_ref[...]))
     inject[...] = jnp.sqrt(1.0 - jnp.exp(-jnp.pi / scale_ref[...]))
-    state_ref[...] = prev_ref[...]
-
-    for part in range(parts):
+
+    for part in range(kinds):
         pltpu.make_async_copy(wide.at[part], wide.at[part], in_sem.at[part]).wait()
         share = reach // rows
         for block in range(blocks):
@@ -137,83 +170,86 @@
                 jnp.bfloat16
             ).reshape(share, rows, slim)
 
-        pair, span = columns(part, me)
+        plane, span = columns(me)
 
         @pl.loop(0, count - 1)
         def _(step):
-            peer = peer_of(step, me, count)
+            peer = peer_at(step, me, count)
+            far = (peer // half + ours) % 2
             pltpu.make_async_remote_copy(
                 src_ref=summed.at[part, peer],
-                dst_ref=back.at[pair, :, span],
+                dst_ref=back.at[part, plane, :, span],
                 send_sem=back_out_sem.at[part],
-                recv_sem=back_in_sem.at[part, (peer // half + ours) % 2],
+                recv_sem=back_in_sem.at[part, far],
                 device_id=(peer,),
                 device_id_type=MESH,
             ).start()
 
         pltpu.make_async_copy(
-            summed.at[part, me], back.at[pair, :, span], back_in_sem.at[part, 0]
+            summed.at[part, me], back.at[part, plane, :, span], back_in_sem.at[part, 0]
         ).start()
 
     def finish(part, at, filtered):
-        for local in range(group):
-            pair = part * group + local
-            component = pair % 3
-            one = pl.ds(component, 1)
-            new = decay[one, at] * state_ref[component, :, at] + inject[one, at] * filtered[local]
-            state_ref[component, :, at] = new
-            if component == 0:
-                value = mean_ref[:, at] + diag_ref[0:1, at] * new
-            elif component == 1:
-                value = off_ref[0:1, at] * state_ref[0, :, at] + diag_ref[1:2, at] * new
+        one = pl.ds(part, 1)
+        state = state_ref[part, :, at]
+        values = []
+        for plane in range(planes):
+            state = decay[one, at] * state + inject[one, at] * filtered[plane]
+            if part == 0:
+                along[plane, :, at] = state
+                value = mean_ref[:, at] + diag_ref[0:1, at] * state
+            elif part == 1:
+                normal[plane, :, at] = state
+                value = off_ref[0:1, at] * along[plane, :, at] + diag_ref[1:2, at] * state
             else:
                 value = (
-                    off_ref[1:2, at] * state_ref[0, :, at]
-                    + off_ref[2:3, at] * state_ref[1, :, at]
-                    + diag_ref[2:3, at] * new
+                    off_ref[1:2, at] * along[plane, :, at]
+                    + off_ref[2:3, at] * normal[plane, :, at]
+                    + diag_ref[2:3, at] * state
                 )
-            vel_ref[pair, :, at] = value.astype(jnp.bfloat16)
-
-    wall_copy.wait()
+            values.append(value)
+        state_ref[part, :, at] = state
+        vel_ref[:, part, :, at] = jnp.stack(values, axis=1).astype(jnp.bfloat16)
+
     tile = min(256, width)
-    for part in range(parts):
-        held = back.at[part * group : (part + 1) * group]
+    for part in range(kinds):
+        held = back.at[part]
+        last = part == kinds - 1
         for far in range(2):
             first = pl.multiple_of((ours + far) % 2 * (width // 2), width // 2)
             span = pl.ds(first, width // 2)
             mine = held.at[:, :, 0 : width // 2]
             pltpu.make_async_copy(mine, mine, back_in_sem.at[part, far]).wait()
-            if part < parts - 1 and far == 0:
+            if not last and far == 0:
                 continue
 
             @pl.loop(0, width // tile)
             def _(step):
                 at = pl.ds(pl.multiple_of(step * tile, tile), tile)
-                reading = span if part == parts - 1 else slice(None)
+                reading = span if last else slice(None)
                 filtered = lax.dot_general(
-                    held[:, :, reading].reshape(group * rows, -1),
+                    held[:, :, reading].reshape(planes * rows, -1),
                     wall[at, reading],
                     (((1,), (1,)), ((), ())),
                     preferred_element_type=jnp.float32,
-                ).reshape(group, rows, tile)
+                ).reshape(planes, rows, tile)
                 if far == 0:
                     early[:, :, at] = filtered
                 else:
-                    if part == parts - 1:
+                    if last:
                         filtered += early[:, :, at]
                     finish(part, at, filtered)
 
-    for part in range(parts):
+    for part in range(kinds):
         sent = wide.at[part, 0 : count - 1]
         pltpu.make_async_copy(sent, sent, out_sem.at[part]).wait()
         pltpu.make_async_copy(sent, sent, back_out_sem.at[part]).wait()
 
 
-def fits(count, rows, pairs, width, reach, slim):
-    columns = pairs * width
+def fits(count, rows, planes, kinds, width, reach, slim):
     return (
-        columns % (count * slim) == 0
-        and (count * slim) % width == 0
+        planes * width == count * slim
+        and kinds == 3
         and width % (2 * slim) == 0
         and count % 2 == 0
         and rows % 16 == 0
@@ -236,39 +272,10 @@
 ):
     count = lax.axis_size("span")
     rows, planes, kinds, width = random_slabs.shape
-    pairs = planes * kinds
     reach = (span_weights.shape[0] - 1) // 2
     slim = LANES
-    parts = pairs * width // (count * slim)
-    x = random_slabs.transpose(0, 2, 1, 3)
-    in_vmem = pl.BlockSpec(memory_space=pltpu.VMEM)
-    velocity, state = pl.pallas_call(
-        functools.partial(exchange_kernel, count, rows, width, pairs, parts, slim, reach),
-        out_shape=(
-            jax.ShapeDtypeStruct((pairs, rows, width), jnp.bfloat16),
-            jax.ShapeDtypeStruct((kinds, rows, width), jnp.float32),
-        ),
-        in_specs=[in_vmem, in_vmem, pl.BlockSpec(memory_space=pl.ANY)] + [in_vmem] * 5,
-        out_specs=(in_vmem, in_vmem),
-        scratch_shapes=[
-            pltpu.VMEM((pairs, rows, width), jnp.bfloat16),
-            pltpu.VMEM((parts, count, rows, slim), jnp.bfloat16),
-            pltpu.VMEM((parts, count, rows, slim), jnp.bfloat16),
-            pltpu.VMEM((pairs, rows, width), jnp.bfloat16),
-            pltpu.VMEM((reach, 3 * reach), jnp.bfloat16),
-            pltpu.VMEM((width, width), jnp.bfloat16),
-            pltpu.VMEM((pairs // parts, rows, width), jnp.float32),
-            pltpu.VMEM((kinds, width), jnp.float32),
-            pltpu.VMEM((kinds, width), jnp.float32),
-            pltpu.SemaphoreType.DMA,
-            pltpu.SemaphoreType.DMA((parts,)),
-            pltpu.SemaphoreType.DMA((parts,)),
-            pltpu.SemaphoreType.DMA((parts,)),
-            pltpu.SemaphoreType.DMA((parts, 2)),
-        ],
-        compiler_params=pltpu.CompilerParams(collective_id=0, has_side_effects=True),
-    )(
-        x,
+    operands = (
+        random_slabs.transpose(0, 2, 1, 3),
         span_weights,
         wall_filter,
         prev_state.transpose(1, 0, 2),
@@ -277,8 +284,48 @@
         lund_diag,
         lund_off,
     )
-    velocity = velocity.reshape(planes, kinds, rows, width).transpose(2, 0, 1, 3)
-    return velocity, state.transpose(1, 0, 2)
+    operands = [pltpu.with_memory_space_constraint(each, pltpu.HBM) for each in operands]
+    in_vmem = pl.BlockSpec(memory_space=pltpu.VMEM)
+    in_hbm = pl.BlockSpec(memory_space=pltpu.HBM)
+    fine = (kinds, width)
+    velocity, state = pl.pallas_call(
+        functools.partial(exchange_kernel, count, rows, width, planes, kinds, slim, reach),
+        out_shape=(
+            pltpu.VMEM((rows, kinds, planes, width), jnp.bfloat16),
+            pltpu.VMEM((kinds, rows, width), jnp.float32),
+        ),
+        in_specs=[in_hbm] * len(operands),
+        out_specs=(in_vmem, in_vmem),
+        scratch_shapes=[
+            pltpu.VMEM((kinds, rows, planes, width), jnp.bfloat16),
+            pltpu.VMEM(span_weights.shape, jnp.float32),
+            pltpu.VMEM(fine, jnp.float32),
+            pltpu.VMEM((1, width), jnp.float32),
+            pltpu.VMEM(fine, jnp.float32),
+            pltpu.VMEM(fine, jnp.float32),
+            pltpu.VMEM((kinds, planes, rows, width), jnp.bfloat16),
+            pltpu.VMEM((kinds, count, rows, slim), jnp.bfloat16),
+            pltpu.VMEM((kinds, count, rows, slim), jnp.bfloat16),
+            pltpu.VMEM((kinds, planes, rows, width), jnp.bfloat16),
+            pltpu.VMEM((reach, 3 * reach), jnp.bfloat16),
+            pltpu.VMEM((width, width), jnp.bfloat16),
+            pltpu.VMEM((planes, rows, width), jnp.float32),
+            pltpu.VMEM((planes, rows, width), jnp.float32),
+            pltpu.VMEM((planes, rows, width), jnp.float32),
+            pltpu.VMEM(fine, jnp.float32),
+            pltpu.VMEM(fine, jnp.float32),
+            pltpu.SemaphoreType.DMA((7,)),
+            pltpu.SemaphoreType.DMA((kinds,)),
+            pltpu.SemaphoreType.DMA((kinds,)),
+            pltpu.SemaphoreType.DMA((kinds,)),
+            pltpu.SemaphoreType.DMA((kinds,)),
+            pltpu.SemaphoreType.DMA((kinds, 2)),
+        ],
+        compiler_params=pltpu.CompilerParams(
+            collective_id=0, has_side_effects=True, vmem_limit_bytes=GRANT
+        ),
+    )(*operands)
+    return velocity.transpose(0, 2, 1, 3), state.transpose(1, 0, 2)
 
 
 def from_partner(value, axis, bit):
@@ -332,7 +379,7 @@
     width = random_slabs.shape[3]
     columns = planes * 3 * width
     half = (span_weights.shape[0] - 1) // 2
-    if fits(lax.axis_size("span"), rows, planes * 3, width, half, LANES):
+    if fits(lax.axis_size("span"), rows, planes, 3, width, half, LANES):
         return exchanged(
             random_slabs,
             span_weights,

time: 87.3 us -> 83.8 us (0.960)
  local copies, waits for them, and re-layouts: 4.72 us -> 2.02 us
    reshape x1 -> x0, local copies, waits for them, and re-layouts: 3.84 us -> none  [exchanged(): velocity.reshape(planes, kinds, rows, width).transpose(2, 0, 1, 3)]
    unnamed x3 -> x2, local copies, waits for them, and re-layouts: 0.88 us -> 2.02 us
where the time goes in v1:
time: 83.8 us; the launch traced here: 83.7 us
  Pallas kernels  81 us (97%)
  local copies, waits for them, and re-layouts  2.02 us (2%)
    pallas_call x1, Pallas kernels, exchanged(): pl.pallas_call(functools.partial(exchange_kernel, count, rows, width, pla...  81 us
    unnamed x2, local copies, waits for them, and re-layouts  2.02 us

profile of v1, /device:TPU:0, one launch (start us, length us, event | category | flops | bytes accessed | tf_op | source)
XLA Modules:
  0.0 83.7 jit_solution(9199865453858963296)
XLA Ops:
  0.6 81.0 %shard_map.95 = (bf16[32,3,4,2048]{3,2,1,0:T(4,128)(2,1)S(1)}, f32[3,32,2048]{2,1,0:T(8,128)S(1)}) custom-call(bf16[32,3,4,2048]{3,2,1,0:T(4,128)(2,1)} %bitcast.7, f32[513]{0:T(1024)} %taps_hbm.1, bf16[2048,2048]{1,0:T(8,128)(2,1)} %wall_hbm.1, f32[3,32,2048]{2,1,0:T(8,128)} %bitcast.8, f32[3,2048]{1,0:T(4,128)} %scale_hbm.1, f32[1,2048]{1,0:T(1,128)} %bitcast.9, ...), custom_call_target="tpu_custom_call" | custom-call | tf_op jit(solution)/shard_map/pallas_call | solution.py:291
  81.7 1.1 %copy.12 = bf16[32,4,3,2048]{3,1,2,0:T(4,128)(2,1)} copy(bf16[32,4,3,2048]{3,1,2,0:T(4,128)(2,1)S(1)} %bitcast.5) | data formatting | bytes 3145728
  82.8 0.9 %copy.13 = f32[32,3,2048]{2,0,1:T(8,128)} copy(f32[32,3,2048]{2,0,1:T(8,128)S(1)} %bitcast.6) | data formatting | bytes 1572864

commit v2 on v1

--- a/solution.py
+++ b/solution.py
@@ -8,11 +8,26 @@
 from jax.sharding import PartitionSpec as P
 
 LANES = 256
-GRANT = 32 << 20
+GRANT = 44 << 20
 MESH = pl.DeviceIdType.MESH
 
 
-def peer_at(step, me, count):
+def peer_at(step, me, count, near_first=False):
+    half, fourth, chips = count // 2, count // 4, count // 8
+    if near_first:
+        near, far = step + 1, step - half + 1
+        away = step >= half - 1
+    else:
+        far, near = step // 2, step // 2 + 1
+        away = step % 2 == 0
+    side = 1 - me // half
+    outer = side * 3 + far // fourth * (1 - 2 * side)
+    there = outer * fourth + (me // 2 + far // 2) % chips * 2 + (me + far) % 2
+    here = me // half * half + (me + near) % half
+    return jnp.where(away, there, here)
+
+
+def old_peer_at(step, me, count):
     away = count // 2 + (1 - 2 * (step % 2)) * ((step + 1) // 2)
     return lax.rem(me + away, count)
 
@@ -47,9 +62,10 @@
     back,
     band,
     wall,
-    early,
+    turned,
+    early_normal,
+    early_spanwise,
     along,
-    normal,
     decay,
     inject,
     load_sem,
@@ -61,8 +77,6 @@
 ):
     me = lax.axis_index("span")
     blocks = count * rows // reach
-    half = count // 2
-    ours = me // half
 
     slab_loads = [
         pltpu.make_async_copy(slab_hbm.at[:, kind], slab.at[kind], slab_sem.at[kind])
@@ -104,12 +118,17 @@
     relayout(0)
     pl.semaphore_wait(barrier, count - 1)
 
-    side = width // slim // 2
+    half, chips = count // 2, count // 8
 
     def columns(owner):
-        place = owner % half
-        start = pl.multiple_of((owner // half * side + place % side) * slim, slim)
-        return place // side, pl.ds(start, slim)
+        block = owner // half * chips + owner // 2 % chips
+        plane = owner // (2 * chips) % 2 * 2 + owner % 2
+        return plane, pl.ds(pl.multiple_of(block * slim, slim), slim)
+
+    def batch(part, sender, receiver):
+        late = (receiver // 2 - sender // 2 + chips) % chips
+        far = jnp.where(sender // half == receiver // half, 0, 1 + late // (chips // 2))
+        return (0, jnp.minimum(far, 1), far)[part]
 
     for part in range(kinds):
         if part:
@@ -117,7 +136,7 @@
 
         @pl.loop(0, count - 1)
         def _(step):
-            peer = peer_at(step, me, count)
+            peer = old_peer_at(step, me, count)
             plane, span = columns(peer)
             pltpu.make_async_remote_copy(
                 src_ref=x_ref.at[part, plane, :, span],
@@ -149,6 +168,16 @@
         first = pl.multiple_of(step * 16, 16)
         rolled = pltpu.roll(tall, first, 1)
         band[pl.ds(first, 16), :] = rolled.astype(jnp.bfloat16)
+
+    piece = min(256, width)
+
+    @pl.loop(0, width // piece)
+    def _(down):
+        @pl.loop(0, width // piece)
+        def _(over):
+            here = pl.ds(pl.multiple_of(down * piece, piece), piece)
+            there = pl.ds(pl.multiple_of(over * piece, piece), piece)
+            turned[there, here] = wall[here, there].T
 
     decay[...] = jnp.exp(-jnp.pi / (2.0 * scale_ref[...]))
     inject[...] = jnp.sqrt(1.0 - jnp.exp(-jnp.pi / scale_ref[...]))
@@ -174,13 +203,13 @@
 
         @pl.loop(0, count - 1)
         def _(step):
-            peer = peer_at(step, me, count)
-            far = (peer // half + ours) % 2
+            peer = peer_at(step, me, count, True) if part == kinds - 1 else old_peer_at(step, me, count)
+            arrival = batch(part, me, peer)
             pltpu.make_async_remote_copy(
                 src_ref=summed.at[part, peer],
                 dst_ref=back.at[part, plane, :, span],
                 send_sem=back_out_sem.at[part],
-                recv_sem=back_in_sem.at[part, far],
+                recv_sem=back_in_sem.at[part, arrival],
                 device_id=(peer,),
                 device_id_type=MESH,
             ).start()
@@ -189,56 +218,96 @@
             summed.at[part, me], back.at[part, plane, :, span], back_in_sem.at[part, 0]
         ).start()
 
-    def finish(part, at, filtered):
+    def advance(part, at, filtered):
         one = pl.ds(part, 1)
         state = state_ref[part, :, at]
-        values = []
+        states = []
         for plane in range(planes):
             state = decay[one, at] * state + inject[one, at] * filtered[plane]
-            if part == 0:
-                along[plane, :, at] = state
-                value = mean_ref[:, at] + diag_ref[0:1, at] * state
-            elif part == 1:
-                normal[plane, :, at] = state
-                value = off_ref[0:1, at] * along[plane, :, at] + diag_ref[1:2, at] * state
-            else:
-                value = (
-                    off_ref[1:2, at] * along[plane, :, at]
-                    + off_ref[2:3, at] * normal[plane, :, at]
-                    + diag_ref[2:3, at] * state
+            states.append(state)
+        state_ref[part, :, at] = state
+        return states
+
+    def put(part, at, values):
+        vel_ref[:, part, :, at] = jnp.stack(values, axis=1).astype(jnp.bfloat16)
+
+    def put_along(at, filtered):
+        states = advance(0, at, filtered)
+        for plane, state in enumerate(states):
+            along[plane, :, at] = state
+        put(0, at, [mean_ref[:, at] + diag_ref[0:1, at] * state for state in states])
+
+    def put_normal(at, filtered):
+        states = advance(1, at, filtered)
+        values = []
+        for plane, state in enumerate(states):
+            first = along[plane, :, at]
+            values.append(off_ref[0:1, at] * first + diag_ref[1:2, at] * state)
+            along[plane, :, at] = off_ref[1:2, at] * first + off_ref[2:3, at] * state
+        put(1, at, values)
+
+    def base_spanwise(at, filtered):
+        for plane, state in enumerate(advance(2, at, filtered)):
+            along[plane, :, at] += diag_ref[2:3, at] * state
+
+    def put_spanwise(at, filtered):
+        extra = inject[2:3, at] * filtered[0]
+        values = [along[0, :, at] + diag_ref[2:3, at] * extra]
+        for plane in range(1, planes):
+            extra = decay[2:3, at] * extra + inject[2:3, at] * filtered[plane]
+            values.append(along[plane, :, at] + diag_ref[2:3, at] * extra)
+        state_ref[2, :, at] += extra
+        put(2, at, values)
+
+    def arrived(part, arrival, pieces):
+        piece = wide.at[part, 0:pieces]
+        pltpu.make_async_copy(piece, piece, back_in_sem.at[part, arrival]).wait()
+
+    def filtering(part, tile, chunks, early, finish):
+        tile = min(tile, width)
+
+        @pl.loop(0, width // tile)
+        def _(step):
+            at = pl.ds(pl.multiple_of(step * tile, tile), tile)
+            total = None
+            for first, size in chunks:
+                reading = pl.ds(first, size)
+                term = jnp.dot(
+                    back[part, :, :, reading].reshape(planes * rows, size),
+                    turned[reading, at],
+                    preferred_element_type=jnp.float32,
                 )
-            values.append(value)
-        state_ref[part, :, at] = state
-        vel_ref[:, part, :, at] = jnp.stack(values, axis=1).astype(jnp.bfloat16)
-
-    tile = min(256, width)
-    for part in range(kinds):
-        held = back.at[part]
-        last = part == kinds - 1
-        for far in range(2):
-            first = pl.multiple_of((ours + far) % 2 * (width // 2), width // 2)
-            span = pl.ds(first, width // 2)
-            mine = held.at[:, :, 0 : width // 2]
-            pltpu.make_async_copy(mine, mine, back_in_sem.at[part, far]).wait()
-            if not last and far == 0:
-                continue
-
-            @pl.loop(0, width // tile)
-            def _(step):
-                at = pl.ds(pl.multiple_of(step * tile, tile), tile)
-                reading = span if last else slice(None)
-                filtered = lax.dot_general(
-                    held[:, :, reading].reshape(planes * rows, -1),
-                    wall[at, reading],
-                    (((1,), (1,)), ((), ())),
-                    preferred_element_type=jnp.float32,
-                ).reshape(planes, rows, tile)
-                if far == 0:
-                    early[:, :, at] = filtered
-                else:
-                    if last:
-                        filtered += early[:, :, at]
-                    finish(part, at, filtered)
+                total = term if total is None else total + term
+            total = total.reshape(planes, rows, tile)
+            if early is not None:
+                total += early[:, :, at]
+            finish(at, total)
+
+    def keep(early):
+        def run(at, filtered):
+            early[:, :, at] = filtered
+
+        return run
+
+    ours = me // half
+    near = [(pl.multiple_of(ours * (width // 2), width // 2), width // 2)]
+    far = [(pl.multiple_of((1 - ours) * (width // 2), width // 2), width // 2)]
+    turns = [(me // 2 - late + chips) % chips for late in range(chips)]
+    late = [
+        (pl.multiple_of(((1 - ours) * chips + turn) * slim, slim), slim) for turn in turns
+    ]
+    arrived(0, 0, count)
+    filtering(0, 512, [(0, width)], None, put_along)
+    arrived(1, 0, half)
+    filtering(1, 1024, near, None, keep(early_normal))
+    arrived(2, 0, half)
+    filtering(2, 1024, near, None, keep(early_spanwise))
+    arrived(1, 1, half)
+    filtering(1, 1024, far, early_normal, put_normal)
+    arrived(2, 1, half // 2)
+    filtering(2, 1024, late[: chips // 2], early_spanwise, base_spanwise)
+    arrived(2, 2, half // 2)
+    filtering(2, 2048, late[chips // 2 :], None, put_spanwise)
 
     for part in range(kinds):
         sent = wide.at[part, 0 : count - 1]
@@ -250,8 +319,8 @@
     return (
         planes * width == count * slim
         and kinds == 3
-        and width % (2 * slim) == 0
-        and count % 2 == 0
+        and planes == 4
+        and count % 16 == 0
         and rows % 16 == 0
         and reach % rows == 0
         and reach % 128 == 0
@@ -309,6 +378,7 @@
             pltpu.VMEM((kinds, planes, rows, width), jnp.bfloat16),
             pltpu.VMEM((reach, 3 * reach), jnp.bfloat16),
             pltpu.VMEM((width, width), jnp.bfloat16),
+            pltpu.VMEM((width, width), jnp.bfloat16),
             pltpu.VMEM((planes, rows, width), jnp.float32),
             pltpu.VMEM((planes, rows, width), jnp.float32),
             pltpu.VMEM((planes, rows, width), jnp.float32),
@@ -319,7 +389,7 @@
             pltpu.SemaphoreType.DMA((kinds,)),
             pltpu.SemaphoreType.DMA((kinds,)),
             pltpu.SemaphoreType.DMA((kinds,)),
-            pltpu.SemaphoreType.DMA((kinds, 2)),
+            pltpu.SemaphoreType.DMA((kinds, 3)),
         ],
         compiler_params=pltpu.CompilerParams(
             collective_id=0, has_side_effects=True, vmem_limit_bytes=GRANT

time: 83.8 us -> 79.2 us (0.945); the launches traced: 83.7 us -> 78.1 us
  Pallas kernels: 81 us -> 75.5 us
    pallas_call x1, Pallas kernels: 81 us -> 75.5 us  [exchanged(): pl.pallas_call(functools.partial(exchange_kernel, count, rows, width, pla...]
where the time goes in v2:
time: 79.2 us; the launch traced here: 78.1 us
  Pallas kernels  75.5 us (95%)
  local copies, waits for them, and re-layouts  2.02 us (3%)
    pallas_call x1, Pallas kernels, exchanged(): pl.pallas_call(functools.partial(exchange_kernel, count, rows, width, pla...  75.5 us
    unnamed x2, local copies, waits for them, and re-layouts  2.02 us

profile of v2, /device:TPU:0, one launch (start us, length us, event | category | flops | bytes accessed | tf_op | source)
XLA Modules:
  0.0 78.1 jit_solution(6634665426080607688)
XLA Ops:
  0.6 75.5 %shard_map.95 = (bf16[32,3,4,2048]{3,2,1,0:T(4,128)(2,1)S(1)}, f32[3,32,2048]{2,1,0:T(8,128)S(1)}) custom-call(bf16[32,3,4,2048]{3,2,1,0:T(4,128)(2,1)} %bitcast.7, f32[513]{0:T(1024)} %taps_hbm.1, bf16[2048,2048]{1,0:T(8,128)(2,1)} %wall_hbm.1, f32[3,32,2048]{2,1,0:T(8,128)} %bitcast.8, f32[3,2048]{1,0:T(4,128)} %scale_hbm.1, f32[1,2048]{1,0:T(1,128)} %bitcast.9, ...), custom_call_target="tpu_custom_call" | custom-call | tf_op jit(solution)/shard_map/pallas_call | solution.py:360
  76.1 1.1 %copy.12 = bf16[32,4,3,2048]{3,1,2,0:T(4,128)(2,1)} copy(bf16[32,4,3,2048]{3,1,2,0:T(4,128)(2,1)S(1)} %bitcast.5) | data formatting | bytes 3145728
  77.3 0.9 %copy.13 = f32[32,3,2048]{2,0,1:T(8,128)} copy(f32[32,3,2048]{2,0,1:T(8,128)S(1)} %bitcast.6) | data formatting | bytes 1572864

commit v3 on v2

--- a/solution.py
+++ b/solution.py
@@ -21,10 +21,53 @@
         far, near = step // 2, step // 2 + 1
         away = step % 2 == 0
     side = 1 - me // half
-    outer = side * 3 + far // fourth * (1 - 2 * side)
+    outer = side * 2 + far // fourth
     there = outer * fourth + (me // 2 + far // 2) % chips * 2 + (me + far) % 2
     here = me // half * half + (me + near) % half
     return jnp.where(away, there, here)
+
+
+def at_distance(away, me, count):
+    core, chip = me % 2, me // 2
+    layers = count // 8
+    layer, aside, along = me // 8, me // 4 % 2, me // 2 % 2
+    found = [(me + 1 - 2 * core, None)] if away == 1 else []
+    for over in range(1 - layers, layers):
+        for turn_aside in range(2):
+            for turn_along in range(2):
+                if abs(over) + turn_aside + turn_along != away:
+                    continue
+                other = (
+                    chip
+                    + over * 4
+                    + turn_aside * (2 - 4 * aside)
+                    + turn_along * (1 - 2 * along)
+                )
+                valid = (layer + over >= 0) & (layer + over < layers) if over else None
+                found += [(other * 2 + (core + turn) % 2, valid) for turn in range(2)]
+    return found
+
+
+def hops(one, other):
+    return (
+        jnp.abs(one // 8 - other // 8)
+        + jnp.abs(one // 4 % 2 - other // 4 % 2)
+        + jnp.abs(one // 2 % 2 - other // 2 % 2)
+        + jnp.where(one // 2 == other // 2, 1, 0)
+    )
+
+
+def degree(me, count):
+    across = me // 8
+    return 5 + 2 * jnp.where(across > 0, 1, 0) + 2 * jnp.where(across < count // 8 - 1, 1, 0)
+
+
+def visit(away, me, count, run):
+    for peer, valid in at_distance(away, me, count):
+        if valid is None:
+            run(peer)
+        else:
+            pl.when(valid)(functools.partial(run, peer))
 
 
 def old_peer_at(step, me, count):
@@ -68,12 +111,14 @@
     along,
     decay,
     inject,
+    mixed,
     load_sem,
     slab_sem,
     out_sem,
     in_sem,
     back_out_sem,
     back_in_sem,
+    met,
 ):
     me = lax.axis_index("span")
     blocks = count * rows // reach
@@ -99,12 +144,17 @@
     slab_loads[0].start()
     barrier = pltpu.get_barrier_semaphore()
 
-    @pl.loop(0, count - 1)
-    def _(step):
-        pl.semaphore_signal(
-            barrier, inc=1, device_id=(peer_at(step, me, count),), device_id_type=MESH
+    def greet(semaphore):
+        visit(
+            1,
+            me,
+            count,
+            lambda peer: pl.semaphore_signal(
+                semaphore, inc=1, device_id=(peer,), device_id_type=MESH
+            ),
         )
 
+    greet(barrier)
     for load in slab_loads[1:]:
         load.start()
     for load in loads:
@@ -112,11 +162,13 @@
 
     def relayout(kind):
         slab_loads[kind].wait()
-        for plane in range(planes):
-            x_ref[kind, plane] = slab[kind, :, plane, :]
-
-    relayout(0)
-    pl.semaphore_wait(barrier, count - 1)
+        for tile in range(width // 128):
+            lanes = slice(tile * 128, (tile + 1) * 128)
+            mixed[tile] = slab[kind, :, :, lanes].reshape(rows * planes, 128).astype(jnp.float32)
+            for plane in range(planes):
+                x_ref[kind, plane, :, lanes] = mixed[tile, pl.ds(plane, rows, planes), :].astype(
+                    jnp.bfloat16
+                )
 
     half, chips = count // 2, count // 8
 
@@ -130,23 +182,41 @@
         far = jnp.where(sender // half == receiver // half, 0, 1 + late // (chips // 2))
         return (0, jnp.minimum(far, 1), far)[part]
 
-    for part in range(kinds):
-        if part:
-            relayout(part)
+    def give(part, peer):
+        plane, span = columns(peer)
+        pltpu.make_async_remote_copy(
+            src_ref=x_ref.at[part, plane, :, span],
+            dst_ref=wide.at[part, me],
+            send_sem=out_sem.at[part],
+            recv_sem=in_sem.at[part],
+            device_id=(peer,),
+            device_id_type=MESH,
+        ).start()
+
+    rounds = count // 8
+    relayout(0)
+    pl.semaphore_wait(barrier, degree(me, count))
+    for round in range(rounds):
+        greet(met.at[round])
+        visit(round + 1, me, count, functools.partial(give, 0))
+        if round + 1 < kinds:
+            relayout(round + 1)
+        if round == 0:
+            visit(1, me, count, functools.partial(give, round + 1))
+        pl.semaphore_wait(met.at[round], degree(me, count))
+    visit(rounds + 1, me, count, functools.partial(give, 0))
+
+    for part in range(1, kinds):
 
         @pl.loop(0, count - 1)
         def _(step):
             peer = old_peer_at(step, me, count)
-            plane, span = columns(peer)
-            pltpu.make_async_remote_copy(
-                src_ref=x_ref.at[part, plane, :, span],
-                dst_ref=wide.at[part, me],
-                send_sem=out_sem.at[part],
-                recv_sem=in_sem.at[part],
-                device_id=(peer,),
-                device_id_type=MESH,
-            ).start()
-
+            if part == 1:
+                pl.when(hops(me, peer) > 1)(functools.partial(give, part, peer))
+            else:
+                give(part, peer)
+
+    for part in range(kinds):
         plane, span = columns(me)
         pltpu.make_async_copy(
             x_ref.at[part, plane, :, span], wide.at[part, me], in_sem.at[part]
@@ -229,7 +299,14 @@
         return states
 
     def put(part, at, values):
-        vel_ref[:, part, :, at] = jnp.stack(values, axis=1).astype(jnp.bfloat16)
+        for tile in range(values[0].shape[1] // 128):
+            lanes = slice(tile * 128, (tile + 1) * 128)
+            for plane, value in enumerate(values):
+                mixed[tile, pl.ds(plane, rows, planes), :] = value[:, lanes]
+            here = pl.ds(pl.multiple_of(at.start + tile * 128, 128), 128)
+            vel_ref[:, part, :, here] = (
+                mixed[tile].astype(jnp.bfloat16).reshape(rows, planes, 128)
+            )
 
     def put_along(at, filtered):
         states = advance(0, at, filtered)
@@ -313,6 +390,17 @@
         sent = wide.at[part, 0 : count - 1]
         pltpu.make_async_copy(sent, sent, out_sem.at[part]).wait()
         pltpu.make_async_copy(sent, sent, back_out_sem.at[part]).wait()
+
+
+def store_kernel(vel_ref, state_ref, vel_out, state_out, sem):
+    copies = (
+        pltpu.make_async_copy(vel_ref, vel_out, sem.at[0]),
+        pltpu.make_async_copy(state_ref, state_out, sem.at[1]),
+    )
+    for copy in copies:
+        copy.start()
+    for copy in copies:
+        copy.wait()
 
 
 def fits(count, rows, planes, kinds, width, reach, slim):
@@ -384,17 +472,30 @@
             pltpu.VMEM((planes, rows, width), jnp.float32),
             pltpu.VMEM(fine, jnp.float32),
             pltpu.VMEM(fine, jnp.float32),
+            pltpu.VMEM((width // 128, rows * planes, 128), jnp.float32),
             pltpu.SemaphoreType.DMA((7,)),
             pltpu.SemaphoreType.DMA((kinds,)),
             pltpu.SemaphoreType.DMA((kinds,)),
             pltpu.SemaphoreType.DMA((kinds,)),
             pltpu.SemaphoreType.DMA((kinds,)),
             pltpu.SemaphoreType.DMA((kinds, 3)),
+            pltpu.SemaphoreType.REGULAR((count // 8,)),
         ],
         compiler_params=pltpu.CompilerParams(
             collective_id=0, has_side_effects=True, vmem_limit_bytes=GRANT
         ),
     )(*operands)
+    velocity, state = pl.pallas_call(
+        store_kernel,
+        out_shape=(
+            jax.ShapeDtypeStruct(velocity.shape, velocity.dtype),
+            jax.ShapeDtypeStruct(state.shape, state.dtype),
+        ),
+        in_specs=[in_vmem, in_vmem],
+        out_specs=(in_hbm, in_hbm),
+        scratch_shapes=[pltpu.SemaphoreType.DMA((2,))],
+        compiler_params=pltpu.CompilerParams(vmem_limit_bytes=GRANT),
+    )(velocity, state)
     return velocity.transpose(0, 2, 1, 3), state.transpose(1, 0, 2)
 
 

time: 79.2 us -> 76.4 us (0.965)
  local copies, waits for them, and re-layouts: 2.02 us -> 0 us
    unnamed x2 -> x0, local copies, waits for them, and re-layouts: 2.02 us -> none
    pallas_call x1, Pallas kernels: 75.5 us -> 73.5 us  [exchanged(): pl.pallas_call(functools.partial(exchange_kernel, count, rows, width, pla...]
    pallas_call x0 -> x1, Pallas kernels: none -> 1.42 us  [exchanged(): pl.pallas_call(store_kernel, out_shape=(jax.ShapeDtypeStruct(velocity.sha...]
where the time goes in v3:
time: 76.4 us; the launch traced here: 75.6 us
  Pallas kernels  75 us (98%)
    pallas_call x1, Pallas kernels, exchanged(): pl.pallas_call(functools.partial(exchange_kernel, count, rows, width, pla...  73.5 us

profile of v3, /device:TPU:0, one launch (start us, length us, event | category | flops | bytes accessed | tf_op | source)
XLA Modules:
  0.0 75.6 jit_solution(11282451480415983707)
XLA Ops:
  0.6 73.5 %shard_map.95 = (bf16[32,3,4,2048]{3,2,1,0:T(4,128)(2,1)S(1)}, f32[3,32,2048]{2,1,0:T(8,128)S(1)}) custom-call(bf16[32,3,4,2048]{3,2,1,0:T(4,128)(2,1)} %bitcast.5, f32[513]{0:T(1024)} %taps_hbm.1, bf16[2048,2048]{1,0:T(8,128)(2,1)} %wall_hbm.1, f32[3,32,2048]{2,1,0:T(8,128)} %bitcast.6, f32[3,2048]{1,0:T(4,128)} %scale_hbm.1, f32[1,2048]{1,0:T(1,128)} %bitcast.7, ...), custom_call_target="tpu_custom_call" | custom-call | tf_op jit(solution)/shard_map/pallas_call | solution.py:448
  74.2 1.4 %shard_map.96 = (bf16[32,3,4,2048]{3,2,1,0:T(4,128)(2,1)}, f32[3,32,2048]{2,1,0:T(8,128)}) custom-call(bf16[32,3,4,2048]{3,2,1,0:T(4,128)(2,1)S(1)} %get-tuple-element.6.vel_ref, f32[3,32,2048]{2,1,0:T(8,128)S(1)} %get-tuple-element.7.state_ref), custom_call_target="tpu_custom_call" | custom-call | tf_op jit(solution)/shard_map/pallas_call | solution.py:488

commit v4 on v3

--- a/solution.py
+++ b/solution.py
@@ -9,6 +9,7 @@
 
 LANES = 256
 GRANT = 44 << 20
+CUTS = 2
 MESH = pl.DeviceIdType.MESH
 
 
@@ -75,6 +76,16 @@
     return lax.rem(me + away, count)
 
 
+def weave(target, mixed, at, values):
+    planes, rows = len(values), values[0].shape[0]
+    for tile in range(values[0].shape[1] // 128):
+        lanes = slice(tile * 128, (tile + 1) * 128)
+        for plane, value in enumerate(values):
+            mixed[tile, pl.ds(plane, rows, planes), :] = value[:, lanes]
+        here = pl.ds(pl.multiple_of(at.start + tile * 128, 128), 128)
+        target[:, :, here] = mixed[tile].astype(jnp.bfloat16).reshape(rows, planes, 128)
+
+
 def exchange_kernel(
     count,
     rows,
@@ -93,6 +104,10 @@
     off_hbm,
     vel_ref,
     state_ref,
+    along,
+    tail_ref,
+    tail_wall_ref,
+    tail_factors_ref,
     slab,
     taps_ref,
     scale_ref,
@@ -108,7 +123,6 @@
     turned,
     early_normal,
     early_spanwise,
-    along,
     decay,
     inject,
     mixed,
@@ -298,21 +312,11 @@
         state_ref[part, :, at] = state
         return states
 
-    def put(part, at, values):
-        for tile in range(values[0].shape[1] // 128):
-            lanes = slice(tile * 128, (tile + 1) * 128)
-            for plane, value in enumerate(values):
-                mixed[tile, pl.ds(plane, rows, planes), :] = value[:, lanes]
-            here = pl.ds(pl.multiple_of(at.start + tile * 128, 128), 128)
-            vel_ref[:, part, :, here] = (
-                mixed[tile].astype(jnp.bfloat16).reshape(rows, planes, 128)
-            )
-
     def put_along(at, filtered):
         states = advance(0, at, filtered)
         for plane, state in enumerate(states):
             along[plane, :, at] = state
-        put(0, at, [mean_ref[:, at] + diag_ref[0:1, at] * state for state in states])
+        weave(vel_ref.at[:, 0], mixed, at, [mean_ref[:, at] + diag_ref[0:1, at] * state for state in states])
 
     def put_normal(at, filtered):
         states = advance(1, at, filtered)
@@ -321,20 +325,11 @@
             first = along[plane, :, at]
             values.append(off_ref[0:1, at] * first + diag_ref[1:2, at] * state)
             along[plane, :, at] = off_ref[1:2, at] * first + off_ref[2:3, at] * state
-        put(1, at, values)
+        weave(vel_ref.at[:, 1], mixed, at, values)
 
     def base_spanwise(at, filtered):
         for plane, state in enumerate(advance(2, at, filtered)):
             along[plane, :, at] += diag_ref[2:3, at] * state
-
-    def put_spanwise(at, filtered):
-        extra = inject[2:3, at] * filtered[0]
-        values = [along[0, :, at] + diag_ref[2:3, at] * extra]
-        for plane in range(1, planes):
-            extra = decay[2:3, at] * extra + inject[2:3, at] * filtered[plane]
-            values.append(along[plane, :, at] + diag_ref[2:3, at] * extra)
-        state_ref[2, :, at] += extra
-        put(2, at, values)
 
     def arrived(part, arrival, pieces):
         piece = wide.at[part, 0:pieces]
@@ -373,6 +368,10 @@
     late = [
         (pl.multiple_of(((1 - ours) * chips + turn) * slim, slim), slim) for turn in turns
     ]
+    for at, (first, size) in enumerate(late[chips // 2 :]):
+        tail_wall_ref[at * slim : (at + 1) * slim] = turned[pl.ds(first, size)]
+    for at, source in enumerate((decay, inject, diag_ref)):
+        tail_factors_ref[at : at + 1] = source[2:3]
     arrived(0, 0, count)
     filtering(0, 512, [(0, width)], None, put_along)
     arrived(1, 0, half)
@@ -384,7 +383,10 @@
     arrived(2, 1, half // 2)
     filtering(2, 1024, late[: chips // 2], early_spanwise, base_spanwise)
     arrived(2, 2, half // 2)
-    filtering(2, 2048, late[chips // 2 :], None, put_spanwise)
+    for at, (first, size) in enumerate(late[chips // 2 :]):
+        tail_ref[:, at * slim : (at + 1) * slim] = back[2, :, :, pl.ds(first, size)].reshape(
+            planes * rows, size
+        )
 
     for part in range(kinds):
         sent = wide.at[part, 0 : count - 1]
@@ -392,13 +394,53 @@
         pltpu.make_async_copy(sent, sent, back_out_sem.at[part]).wait()
 
 
-def store_kernel(vel_ref, state_ref, vel_out, state_out, sem):
-    copies = (
-        pltpu.make_async_copy(vel_ref, vel_out, sem.at[0]),
-        pltpu.make_async_copy(state_ref, state_out, sem.at[1]),
-    )
+def store_kernel(
+    vel_ref,
+    state_ref,
+    base_ref,
+    tail_ref,
+    wall_ref,
+    factors_ref,
+    vel_out,
+    state_out,
+    last,
+    last_state,
+    mixed,
+    sem,
+):
+    planes, rows, width = base_ref.shape
+    kinds = state_ref.shape[0]
+    ready = pl.ds(0, kinds - 1)
+    copies = [
+        pltpu.make_async_copy(vel_ref, vel_out.at[:, ready], sem.at[0]),
+        pltpu.make_async_copy(state_ref.at[ready], state_out.at[ready], sem.at[1]),
+    ]
     for copy in copies:
         copy.start()
+    tile = width // CUTS
+    for cut in range(CUTS):
+        at = pl.ds(cut * tile, tile)
+        filtered = jnp.dot(
+            tail_ref[...], wall_ref[:, at], preferred_element_type=jnp.float32
+        ).reshape(planes, rows, tile)
+        decay, inject, diag = (factors_ref[one : one + 1, at] for one in range(3))
+        extra = inject * filtered[0]
+        values = [base_ref[0, :, at] + diag * extra]
+        for plane in range(1, planes):
+            extra = decay * extra + inject * filtered[plane]
+            values.append(base_ref[plane, :, at] + diag * extra)
+        last_state[:, at] = state_ref[kinds - 1, :, at] + extra
+        weave(last, mixed, at, values)
+        copies += [
+            pltpu.make_async_copy(
+                last.at[:, :, at], vel_out.at[:, kinds - 1, :, at], sem.at[2 + 2 * cut]
+            ),
+            pltpu.make_async_copy(
+                last_state.at[:, at], state_out.at[kinds - 1, :, at], sem.at[3 + 2 * cut]
+            ),
+        ]
+        for copy in copies[-2:]:
+            copy.start()
     for copy in copies:
         copy.wait()
 
@@ -445,14 +487,18 @@
     in_vmem = pl.BlockSpec(memory_space=pltpu.VMEM)
     in_hbm = pl.BlockSpec(memory_space=pltpu.HBM)
     fine = (kinds, width)
-    velocity, state = pl.pallas_call(
+    held = pl.pallas_call(
         functools.partial(exchange_kernel, count, rows, width, planes, kinds, slim, reach),
         out_shape=(
-            pltpu.VMEM((rows, kinds, planes, width), jnp.bfloat16),
+            pltpu.VMEM((rows, kinds - 1, planes, width), jnp.bfloat16),
             pltpu.VMEM((kinds, rows, width), jnp.float32),
+            pltpu.VMEM((planes, rows, width), jnp.float32),
+            pltpu.VMEM((planes * rows, width // 4), jnp.bfloat16),
+            pltpu.VMEM((width // 4, width), jnp.bfloat16),
+            pltpu.VMEM(fine, jnp.float32),
         ),
         in_specs=[in_hbm] * len(operands),
-        out_specs=(in_vmem, in_vmem),
+        out_specs=(in_vmem,) * 6,
         scratch_shapes=[
             pltpu.VMEM((kinds, rows, planes, width), jnp.bfloat16),
             pltpu.VMEM(span_weights.shape, jnp.float32),
@@ -467,7 +513,6 @@
             pltpu.VMEM((reach, 3 * reach), jnp.bfloat16),
             pltpu.VMEM((width, width), jnp.bfloat16),
             pltpu.VMEM((width, width), jnp.bfloat16),
-            pltpu.VMEM((planes, rows, width), jnp.float32),
             pltpu.VMEM((planes, rows, width), jnp.float32),
             pltpu.VMEM((planes, rows, width), jnp.float32),
             pltpu.VMEM(fine, jnp.float32),
@@ -488,14 +533,19 @@
     velocity, state = pl.pallas_call(
         store_kernel,
         out_shape=(
-            jax.ShapeDtypeStruct(velocity.shape, velocity.dtype),
-            jax.ShapeDtypeStruct(state.shape, state.dtype),
+            jax.ShapeDtypeStruct((rows, kinds, planes, width), jnp.bfloat16),
+            jax.ShapeDtypeStruct((kinds, rows, width), jnp.float32),
         ),
-        in_specs=[in_vmem, in_vmem],
+        in_specs=[in_vmem] * len(held),
         out_specs=(in_hbm, in_hbm),
-        scratch_shapes=[pltpu.SemaphoreType.DMA((2,))],
-        compiler_params=pltpu.CompilerParams(vmem_limit_bytes=GRANT),
-    )(velocity, state)
+        scratch_shapes=[
+            pltpu.VMEM((rows, planes, width), jnp.bfloat16),
+            pltpu.VMEM((rows, width), jnp.float32),
+            pltpu.VMEM((width // 128, rows * planes, 128), jnp.float32),
+            pltpu.SemaphoreType.DMA((2 + 2 * CUTS,)),
+        ],
+        compiler_params=pltpu.CompilerParams(vmem_limit_bytes=GRANT // 2),
+    )(*held)
     return velocity.transpose(0, 2, 1, 3), state.transpose(1, 0, 2)
 
 

time: 76.4 us -> 75.8 us (level)
  no operation moved by 1% of the time
where the time goes in v4:
time: 75.8 us; the launch traced here: 75 us
  Pallas kernels  74.3 us (98%)
    pallas_call x1, Pallas kernels, exchanged(): pl.pallas_call(functools.partial(exchange_kernel, count, rows, width, pla...  72.9 us

profile of v4, /device:TPU:0, one launch (start us, length us, event | category | flops | bytes accessed | tf_op | source)
XLA Modules:
  0.0 75.0 jit_solution(978403064797641224)
XLA Ops:
  0.6 72.9 %shard_map.95 = (bf16[32,2,4,2048]{3,2,1,0:T(4,128)(2,1)S(1)}, f32[3,32,2048]{2,1,0:T(8,128)S(1)}, f32[4,32,2048]{2,1,0:T(8,128)S(1)}, bf16[128,512]{1,0:T(8,128...) custom-call(bf16[32,3,4,2048]{3,2,1,0:T(4,128)(2,1)} %bitcast.5, f32[513]{0:T(1024)} %taps_hbm.1, ...), custom_call_target="tpu_custom_call" | custom-call | tf_op jit(solution)/shard_map/pallas_call | solution.py:490
  73.5 1.5 %shard_map.96 = (bf16[32,3,4,2048]{3,2,1,0:T(4,128)(2,1)}, f32[3,32,2048]{2,1,0:T(8,128)}) custom-call(bf16[32,2,4,2048]{3,2,1,0:T(4,128)(2,1)S(1)} %get-tuple-element.10.vel_ref, f32[3,32,2048]{2,1,0:T(8,128)S(1)} %get-tuple-element.11.state_ref, f32[4,32,2048]{2,1,0:T(8,128)S(1)} %get-tuple-element.12.base_ref, ...), custom_call_target="tpu_custom_call" | custom-call | tf_op jit(solution)/shard_map/pallas_call | solution.py:533

commit v5 on v4

--- a/solution.py
+++ b/solution.py
@@ -178,9 +178,10 @@
         slab_loads[kind].wait()
         for tile in range(width // 128):
             lanes = slice(tile * 128, (tile + 1) * 128)
+            block_lanes = slice(tile * 128 % slim, tile * 128 % slim + 128)
             mixed[tile] = slab[kind, :, :, lanes].reshape(rows * planes, 128).astype(jnp.float32)
             for plane in range(planes):
-                x_ref[kind, plane, :, lanes] = mixed[tile, pl.ds(plane, rows, planes), :].astype(
+                x_ref[kind, plane, tile * 128 // slim, :, block_lanes] = mixed[tile, pl.ds(plane, rows, planes), :].astype(
                     jnp.bfloat16
                 )
 
@@ -189,17 +190,17 @@
     def columns(owner):
         block = owner // half * chips + owner // 2 % chips
         plane = owner // (2 * chips) % 2 * 2 + owner % 2
-        return plane, pl.ds(pl.multiple_of(block * slim, slim), slim)
+        return plane, block
 
     def batch(part, sender, receiver):
         late = (receiver // 2 - sender // 2 + chips) % chips
-        far = jnp.where(sender // half == receiver // half, 0, 1 + late // (chips // 2))
+        far = jnp.where(sender // half == receiver // half, 0, 1 + jnp.minimum(late, 1))
         return (0, jnp.minimum(far, 1), far)[part]
 
     def give(part, peer):
         plane, span = columns(peer)
         pltpu.make_async_remote_copy(
-            src_ref=x_ref.at[part, plane, :, span],
+            src_ref=x_ref.at[part, plane, span],
             dst_ref=wide.at[part, me],
             send_sem=out_sem.at[part],
             recv_sem=in_sem.at[part],
@@ -233,7 +234,7 @@
     for part in range(kinds):
         plane, span = columns(me)
         pltpu.make_async_copy(
-            x_ref.at[part, plane, :, span], wide.at[part, me], in_sem.at[part]
+            x_ref.at[part, plane, span], wide.at[part, me], in_sem.at[part]
         ).start()
 
     for load in loads:
@@ -287,11 +288,11 @@
 
         @pl.loop(0, count - 1)
         def _(step):
-            peer = peer_at(step, me, count, True) if part == kinds - 1 else old_peer_at(step, me, count)
+            peer = peer_at(step, me, count) if part == kinds - 1 else old_peer_at(step, me, count)
             arrival = batch(part, me, peer)
             pltpu.make_async_remote_copy(
                 src_ref=summed.at[part, peer],
-                dst_ref=back.at[part, plane, :, span],
+                dst_ref=back.at[part, plane, span],
                 send_sem=back_out_sem.at[part],
                 recv_sem=back_in_sem.at[part, arrival],
                 device_id=(peer,),
@@ -299,7 +300,7 @@
             ).start()
 
         pltpu.make_async_copy(
-            summed.at[part, me], back.at[part, plane, :, span], back_in_sem.at[part, 0]
+            summed.at[part, me], back.at[part, plane, span], back_in_sem.at[part, 0]
         ).start()
 
     def advance(part, at, filtered):
@@ -342,10 +343,10 @@
         def _(step):
             at = pl.ds(pl.multiple_of(step * tile, tile), tile)
             total = None
-            for first, size in chunks:
-                reading = pl.ds(first, size)
+            for first in chunks:
+                reading = pl.ds(pl.multiple_of(first * slim, slim), slim)
                 term = jnp.dot(
-                    back[part, :, :, reading].reshape(planes * rows, size),
+                    back[part, :, first].reshape(planes * rows, slim),
                     turned[reading, at],
                     preferred_element_type=jnp.float32,
                 )
@@ -362,31 +363,29 @@
         return run
 
     ours = me // half
-    near = [(pl.multiple_of(ours * (width // 2), width // 2), width // 2)]
-    far = [(pl.multiple_of((1 - ours) * (width // 2), width // 2), width // 2)]
+    near = [ours * chips + one for one in range(chips)]
+    far = [(1 - ours) * chips + one for one in range(chips)]
     turns = [(me // 2 - late + chips) % chips for late in range(chips)]
-    late = [
-        (pl.multiple_of(((1 - ours) * chips + turn) * slim, slim), slim) for turn in turns
-    ]
-    for at, (first, size) in enumerate(late[chips // 2 :]):
-        tail_wall_ref[at * slim : (at + 1) * slim] = turned[pl.ds(first, size)]
+    late = [(1 - ours) * chips + turn for turn in turns]
+    for at, first in enumerate(late[1:]):
+        tail_wall_ref[at * slim : (at + 1) * slim] = turned[
+            pl.ds(pl.multiple_of(first * slim, slim), slim)
+        ]
     for at, source in enumerate((decay, inject, diag_ref)):
         tail_factors_ref[at : at + 1] = source[2:3]
     arrived(0, 0, count)
-    filtering(0, 512, [(0, width)], None, put_along)
+    filtering(0, 512, list(range(2 * chips)), None, put_along)
     arrived(1, 0, half)
     filtering(1, 1024, near, None, keep(early_normal))
     arrived(2, 0, half)
     filtering(2, 1024, near, None, keep(early_spanwise))
     arrived(1, 1, half)
     filtering(1, 1024, far, early_normal, put_normal)
-    arrived(2, 1, half // 2)
-    filtering(2, 1024, late[: chips // 2], early_spanwise, base_spanwise)
-    arrived(2, 2, half // 2)
-    for at, (first, size) in enumerate(late[chips // 2 :]):
-        tail_ref[:, at * slim : (at + 1) * slim] = back[2, :, :, pl.ds(first, size)].reshape(
-            planes * rows, size
-        )
+    arrived(2, 1, half // chips)
+    filtering(2, 1024, late[:1], early_spanwise, base_spanwise)
+    arrived(2, 2, half - half // chips)
+    for at, first in enumerate(late[1:]):
+        tail_ref[:, at * slim : (at + 1) * slim] = back[2, :, first].reshape(planes * rows, slim)
 
     for part in range(kinds):
         sent = wide.at[part, 0 : count - 1]
@@ -493,8 +492,8 @@
             pltpu.VMEM((rows, kinds - 1, planes, width), jnp.bfloat16),
             pltpu.VMEM((kinds, rows, width), jnp.float32),
             pltpu.VMEM((planes, rows, width), jnp.float32),
-            pltpu.VMEM((planes * rows, width // 4), jnp.bfloat16),
-            pltpu.VMEM((width // 4, width), jnp.bfloat16),
+            pltpu.VMEM((planes * rows, width // 2 - slim), jnp.bfloat16),
+            pltpu.VMEM((width // 2 - slim, width), jnp.bfloat16),
             pltpu.VMEM(fine, jnp.float32),
         ),
         in_specs=[in_hbm] * len(operands),
@@ -506,10 +505,10 @@
             pltpu.VMEM((1, width), jnp.float32),
             pltpu.VMEM(fine, jnp.float32),
             pltpu.VMEM(fine, jnp.float32),
-            pltpu.VMEM((kinds, planes, rows, width), jnp.bfloat16),
+            pltpu.VMEM((kinds, planes, width // slim, rows, slim), jnp.bfloat16),
             pltpu.VMEM((kinds, count, rows, slim), jnp.bfloat16),
             pltpu.VMEM((kinds, count, rows, slim), jnp.bfloat16),
-            pltpu.VMEM((kinds, planes, rows, width), jnp.bfloat16),
+            pltpu.VMEM((kinds, planes, width // slim, rows, slim), jnp.bfloat16),
             pltpu.VMEM((reach, 3 * reach), jnp.bfloat16),
             pltpu.VMEM((width, width), jnp.bfloat16),
             pltpu.VMEM((width, width), jnp.bfloat16),

time: 75.8 us -> 75.4 us (level)
  no operation moved by 1% of the time
where the time goes in v5:
time: 75.4 us; the launch traced here: 75.1 us
  Pallas kernels  74.4 us (99%)
    pallas_call x1, Pallas kernels, exchanged(): pl.pallas_call(functools.partial(exchange_kernel, count, rows, width, pla...  72.9 us
    pallas_call x1, Pallas kernels, exchanged(): pl.pallas_call(store_kernel, out_shape=(jax.ShapeDtypeStruct((rows, kinds...  1.58 us

profile of v5, /device:TPU:0, one launch (start us, length us, event | category | flops | bytes accessed | tf_op | source)
XLA Modules:
  0.0 75.1 jit_solution(7750067320789726665)
XLA Ops:
  0.6 72.9 %shard_map.95 = (bf16[32,2,4,2048]{3,2,1,0:T(4,128)(2,1)S(1)}, f32[3,32,2048]{2,1,0:T(8,128)S(1)}, f32[4,32,2048]{2,1,0:T(8,128)S(1)}, bf16[128,768]{1,0:T(8,128...) custom-call(bf16[32,3,4,2048]{3,2,1,0:T(4,128)(2,1)} %bitcast.5, f32[513]{0:T(1024)} %taps_hbm.1, ...), custom_call_target="tpu_custom_call" | custom-call | tf_op jit(solution)/shard_map/pallas_call | solution.py:489
  73.5 1.6 %shard_map.96 = (bf16[32,3,4,2048]{3,2,1,0:T(4,128)(2,1)}, f32[3,32,2048]{2,1,0:T(8,128)}) custom-call(bf16[32,2,4,2048]{3,2,1,0:T(4,128)(2,1)S(1)} %get-tuple-element.10.vel_ref, f32[3,32,2048]{2,1,0:T(8,128)S(1)} %get-tuple-element.11.state_ref, f32[4,32,2048]{2,1,0:T(8,128)S(1)} %get-tuple-element.12.base_ref, ...), custom_call_target="tpu_custom_call" | custom-call | tf_op jit(solution)/shard_map/pallas_call | solution.py:532
